TPU v7x, 32 devices: a whole 2x2x4 slice. The times are simulated.
32 devices in a mesh: seq: 8 (over y, x, core), head: 4 (over z).
Axes of the slice: x: 2, y: 2, z: 4, core: 2. Of those that a mesh axis runs over, the one named last changes fastest.
Arguments:
- values: bfloat16 [16384, 5120], P('seq', 'head'), may hold values from -6 to 6
- gates: bfloat16 [16384, 5120], P('seq', 'head'), may hold values from -6 to 6
- b_proj: bfloat16 [16384, 128], P('seq'), may hold values from -2 to 2
- c_proj: bfloat16 [16384, 128], P('seq'), may hold values from -2 to 2
- step_size: float32 [80, 16384], P('head', 'seq'), may hold values from 0.006 to 0.06
- decay_rate: float32 [80, 16384], P('head', 'seq'), may hold values from 0 to 1.2, as said below
- skip_gain: float32 [80], P('head'), may hold values from 0.5 to 2
- norm_gain: float32 [5120], P('head'), may hold values from 0.25 to 1.75
- readout_matrix: bfloat16 [5120, 2560], P('head'), may hold values from -0.078125 to 0.078125
- span_counts: int32 [8], P('seq'), may hold values from 1 to 8, as said below
- remaining_count: int32 [8], P('seq'), may hold values from 1 to 256
Outputs:
- mixer_response: bfloat16 [16384, 2560], P(('seq', 'head'))
Inputs may be any that keep to these rules, and one draw needn't show every extreme that they name: `span_counts`: some shard uses all 8 span slots in every draw. `decay_rate`: Positive.
All inputs are finite; a program needn't handle non-finite values.
Results may differ from a plain program's by a relative error of at most 0.02.
Values may be sent and summed in bfloat16 or wider, within the bound.
A program may use at most 192 MiB of HBM per device.

v0:
```python
import functools
import math

import jax
import jax.numpy as jnp
from jax import lax
from jax.experimental import pallas as pl
from jax.experimental.pallas import tpu as pltpu
from jax.sharding import PartitionSpec as P

SPAN = 256
LOG2E = math.log2(math.e)
F32 = jnp.float32
BF16 = jnp.bfloat16
HIGH = lax.Precision.HIGHEST
MESH = pl.DeviceIdType.MESH
VMEM = pltpu.VMEM
LIMIT = 63 * 1024 * 1024
TILE = 256


def contract(a, b, da, db, precision=None):
    return lax.dot_general(
        a, b, (((da,), (db,)), ((), ())), precision=precision, preferred_element_type=F32
    )


def expander(heads, width):
    size = width // heads
    col = lax.broadcasted_iota(jnp.int32, (heads, width), 1) // size
    row = lax.broadcasted_iota(jnp.int32, (heads, width), 0)
    return jnp.where(col == row, 1.0, 0.0).astype(F32)


def halves(a):
    hi = a.astype(BF16)
    return hi, (a - hi.astype(F32)).astype(BF16)


def pack_rows(total):
    total = jnp.broadcast_to(total, (16, total.shape[1]))
    hi, mid = halves(total)
    low = (total - hi.astype(F32) - mid.astype(F32)).astype(BF16)
    row = lax.broadcasted_iota(jnp.int32, total.shape, 0)
    parts = jnp.where(row == 0, hi.astype(F32), jnp.where(row == 1, mid.astype(F32), low.astype(F32)))
    return jnp.where(row < 3, parts, 0.0).astype(BF16)


def unpack_rows(rows):
    rows = rows.astype(F32)
    return rows[0:1, :] + rows[1:2, :] + rows[2:3, :]


def pick(table, index):
    total = jnp.int32(0)
    for i, value in enumerate(table):
        total = total + jnp.where(index == i, jnp.int32(value), jnp.int32(0))
    return total


def near_order(ranks):
    return [sorted((r for r in range(ranks) if r != h), key=lambda r: (abs(r - h), r)) for h in range(ranks)]


def layer_kernel(
    ranks,
    shards,
    count_ref,
    remain_ref,
    skip_ref,
    gain_ref,
    x_hbm,
    g_hbm,
    b_hbm,
    c_hbm,
    st_hbm,
    dr_hbm,
    w_hbm,
    out_hbm,
    x_ref,
    g_ref,
    b_ref,
    c_ref,
    st_ref,
    dr_ref,
    runT_ref,
    q_ref,
    before_ref,
    lead_ref,
    s_ref,
    l_ref,
    mine_ref,
    other_ref,
    chip_ref,
    chips_ref,
    inc_ref,
    w_ref,
    got_ref,
    ss_buf,
    ss_ref,
    acc_ref,
    res_ref,
    x_sem,
    g_sem,
    in_sem,
    w_sem,
    right_s,
    right_r,
    left_s,
    left_r,
    plane_s,
    plane_r,
    sib_s,
    sib_r,
    pair_s,
    pair_r,
    chip_s,
    chip_r,
    send_sem,
    recv_sem,
    ssend_sem,
    srecv_sem,
    out_sem,
):
    heads, length = q_ref.shape
    width = x_ref.shape[1]
    blocks = length // SPAN
    each = blocks // ranks
    share = length // ranks
    state = s_ref.shape[0]
    depth = res_ref.shape[1]
    rows = width // shards
    chips = shards // 2
    half = width // 2
    tiles = depth // TILE
    me = lax.axis_index("head")
    place = lax.axis_index("seq")
    core = lax.rem(place, 2)
    chip = lax.div(place, 2)
    sibling = place + 1 - 2 * core
    valid = (count_ref[0] - 1) * SPAN + remain_ref[0]

    def span_at(c):
        return pl.ds(pl.multiple_of(c * SPAN, SPAN), SPAN)

    def slice_at(owner):
        return pl.ds(pl.multiple_of(owner * rows, rows), rows)

    def load_w(i):
        owner = lax.rem(place + i, shards)
        return pltpu.make_async_copy(
            w_hbm.at[slice_at(owner), :], w_ref.at[me, slice_at(owner), :], w_sem.at[i]
        )

    def load_x(c):
        return pltpu.make_async_copy(x_hbm.at[span_at(c), :], x_ref.at[span_at(c), :], x_sem.at[c])

    def load_g(c):
        return pltpu.make_async_copy(g_hbm.at[span_at(c), :], g_ref.at[span_at(c), :], g_sem.at[c])

    smalls = [
        pltpu.make_async_copy(src, dst, in_sem.at[i])
        for i, (src, dst) in enumerate(
            ((st_hbm, st_ref), (dr_hbm, dr_ref), (b_hbm, b_ref), (c_hbm, c_ref))
        )
    ]

    def along(k, step):
        r = me - step * k
        send, recv = (right_s, right_r) if step > 0 else (left_s, left_r)
        return pltpu.make_async_remote_copy(
            src_ref=w_ref.at[r, slice_at(place), :],
            dst_ref=w_ref.at[r, slice_at(place), :],
            send_sem=send.at[k],
            recv_sem=recv.at[k],
            device_id={"head": me + step},
            device_id_type=MESH,
        )

    def arrived(k, step):
        r = me - step * (k + 1)
        send, recv = (right_s, right_r) if step > 0 else (left_s, left_r)
        return pltpu.make_async_remote_copy(
            src_ref=w_ref.at[r, slice_at(place), :],
            dst_ref=w_ref.at[r, slice_at(place), :],
            send_sem=send.at[k],
            recv_sem=recv.at[k],
            device_id={"head": me - step},
            device_id_type=MESH,
        )

    def plane(r, j):
        slot = lax.rem(r - me + ranks, ranks) - 1
        dest = lax.rem(chip + j, chips) * 2 + core
        return pltpu.make_async_remote_copy(
            src_ref=w_ref.at[r, slice_at(place), :],
            dst_ref=w_ref.at[r, slice_at(place), :],
            send_sem=plane_s.at[slot, j],
            recv_sem=plane_r.at[slot, j],
            device_id={"seq": dest},
            device_id_type=MESH,
        )

    def landed(r, j):
        slot = lax.rem(r - me + ranks, ranks) - 1
        owner = lax.rem(chip - j + chips, chips) * 2 + core
        return pltpu.make_async_remote_copy(
            src_ref=w_ref.at[r, slice_at(owner), :],
            dst_ref=w_ref.at[r, slice_at(owner), :],
            send_sem=plane_s.at[slot, j],
            recv_sem=plane_r.at[slot, j],
            device_id={"seq": owner},
            device_id_type=MESH,
        )

    def across(r, j, of_core):
        slot = lax.rem(r - me + ranks, ranks) - 1
        owner = lax.rem(chip - j + chips, chips) * 2 + of_core
        return pltpu.make_async_remote_copy(
            src_ref=w_ref.at[r, slice_at(owner), :],
            dst_ref=w_ref.at[r, slice_at(owner), :],
            send_sem=sib_s.at[slot, j],
            recv_sem=sib_r.at[slot, j],
            device_id={"seq": sibling},
            device_id_type=MESH,
        )

    def spread_plane(r):
        across(r, 0, core).start()

        def one(j, carry):
            plane(r, j).start()
            return carry

        lax.fori_loop(1, chips, one, 0)

    def relay(k):
        for step in (1, -1):
            source = me - step * k
            last = me == (ranks - 1 if step > 0 else 0)

            @pl.when((source >= 0) & (source < ranks))
            def _(step=step, source=source, last=last):
                arrived(k - 1, step).wait_recv()
                if k < ranks - 1:

                    @pl.when(jnp.logical_not(last))
                    def _():
                        along(k, step).start()

                spread_plane(source)

    load_w(0).start()
    for copy in smalls[:3]:
        copy.start()

    def load_xs(c, carry):
        load_x(c).start()
        return carry

    lax.fori_loop(0, blocks, load_xs, 0)
    smalls[3].start()

    barrier = pltpu.get_barrier_semaphore()

    def greet(k, carry):
        pl.semaphore_signal(
            barrier, inc=1, device_id={"head": lax.rem(me + k, ranks)}, device_id_type=MESH
        )
        return carry

    def greet_plane(j, carry):
        dest = lax.rem(chip + j, chips) * 2 + core
        pl.semaphore_signal(barrier, inc=1, device_id={"seq": dest}, device_id_type=MESH)
        return carry

    lax.fori_loop(1, ranks, greet, 0)
    lax.fori_loop(1, chips, greet_plane, 0)
    pl.semaphore_signal(barrier, inc=1, device_id={"seq": sibling}, device_id_type=MESH)
    pl.semaphore_wait(barrier, ranks - 1 + chips)

    load_w(0).wait()

    @pl.when(me < ranks - 1)
    def _():
        along(0, 1).start()

    @pl.when(me > 0)
    def _():
        along(0, -1).start()

    i0 = lax.broadcasted_iota(jnp.int32, (SPAN, SPAN), 0)
    i1 = lax.broadcasted_iota(jnp.int32, (SPAN, SPAN), 1)
    lower = i0 >= i1
    tril = jnp.where(lower, 1.0, 0.0).astype(F32)
    spread = expander(heads, width)
    spread16 = spread.astype(BF16)
    s_ref[...] = jnp.zeros_like(s_ref)
    l_ref[...] = jnp.ones_like(l_ref)
    for copy in smalls[:3]:
        copy.wait()

    def scan(c, carry):
        at = span_at(c)
        load_x(c).wait()
        load_g(c).start()
        slot = c * SPAN + lax.broadcasted_iota(jnp.int32, (heads, SPAN), 1)
        live = slot < valid
        ld = jnp.where(live, dr_ref[:, at] * (-LOG2E), 0.0)
        run = contract(ld, tril, 1, 1, HIGH)
        runT = contract(tril, ld, 1, 1, HIGH)
        q = jnp.where(live, run - jnp.log2(st_ref[:, at]), 1e30)
        runT_ref[at, :] = runT
        q_ref[:, at] = q
        tail = jnp.exp2(run[:, SPAN - 1 :] - q)
        hi, lo = halves(tail)
        texp = contract(hi, spread16, 0, 0) + contract(lo, spread16, 0, 0)
        weighted = (x_ref[at, :].astype(F32) * texp).astype(BF16)
        fresh = contract(b_ref[at, :], weighted, 0, 0)
        dec = contract(jnp.exp2(runT[SPAN - 8 :, :]), spread, 1, 0, HIGH)[7:8, :]
        before_ref[c] = s_ref[...]
        lead_ref[c] = l_ref[...]
        s_ref[...] = dec * s_ref[...] + fresh
        l_ref[...] = l_ref[...] * dec
        return carry

    lax.fori_loop(0, blocks, scan, 0)
    mine_ref[0:state, :] = s_ref[...].astype(BF16)
    mine_ref[state:, :] = pack_rows(l_ref[0:1, :])

    pair = pltpu.make_async_remote_copy(
        src_ref=mine_ref,
        dst_ref=other_ref,
        send_sem=pair_s.at[0],
        recv_sem=pair_r.at[0],
        device_id={"seq": sibling},
        device_id_type=MESH,
    )
    pair.start()

    def load_ws(i, carry):
        load_w(i).start()
        return carry

    lax.fori_loop(1, shards, load_ws, 0)
    pair.wait()
    cols = pl.ds(pl.multiple_of(core * half, half), half)
    own = mine_ref[:, cols].astype(F32)
    peer = other_ref[:, cols].astype(F32)
    first = jnp.where(core == 0, own, peer)
    second = jnp.where(core == 0, peer, own)
    first_dec = unpack_rows(first[state:, :])
    second_dec = unpack_rows(second[state:, :])
    chip_ref[0:state, :] = (second_dec * first[0:state, :] + second[0:state, :]).astype(BF16)
    chip_ref[state:, :] = pack_rows(first_dec * second_dec)

    def to_chip(j, other):
        return pltpu.make_async_remote_copy(
            src_ref=chip_ref,
            dst_ref=chips_ref.at[j],
            send_sem=chip_s.at[j],
            recv_sem=chip_r.at[j],
            device_id={"seq": other * 2 + core},
            device_id_type=MESH,
        )

    def tell(j, carry):
        @pl.when(chip + j < chips)
        def _():
            to_chip(j, chip + j).start()

        return carry

    lax.fori_loop(1, chips, tell, 0)
    inc_ref[:, cols] = jnp.zeros((state, half), F32)

    def hear(i, carry):
        j = chips - i

        @pl.when(j <= chip)
        def _():
            to_chip(j, chip - j).wait_recv()
            block = chips_ref[j]
            decay = unpack_rows(block[state:, :])
            inc_ref[:, cols] = decay * inc_ref[:, cols] + block[0:state, :].astype(F32)

        return carry

    lax.fori_loop(1, chips, hear, 0)
    swap = pltpu.make_async_remote_copy(
        src_ref=inc_ref.at[:, cols],
        dst_ref=inc_ref.at[:, cols],
        send_sem=pair_s.at[1],
        recv_sem=pair_r.at[1],
        device_id={"seq": sibling},
        device_id_type=MESH,
    )
    swap.start()
    swap.wait()
    inc = inc_ref[...]
    after = unpack_rows(other_ref[state:, :]) * inc + other_ref[0:state, :].astype(F32)
    inc_ref[...] = jnp.where(core == 1, after, inc)

    relay(1)
    smalls[3].wait()
    left = lax.broadcasted_iota(jnp.int32, (SPAN, 128), 1) < (width // heads)
    ones = jnp.ones((8, 128), F32)

    def copies(dest, j, slot):
        c = dest * each + j
        big = pltpu.make_async_remote_copy(
            src_ref=g_ref.at[span_at(c), :],
            dst_ref=got_ref.at[slot, pl.ds(j * SPAN, SPAN), :],
            send_sem=send_sem.at[slot, j],
            recv_sem=recv_sem.at[slot, j],
            device_id={"head": dest},
            device_id_type=MESH,
        )
        small = pltpu.make_async_remote_copy(
            src_ref=ss_buf.at[c],
            dst_ref=ss_ref.at[slot, j],
            send_sem=ssend_sem.at[slot, j],
            recv_sem=srecv_sem.at[slot, j],
            device_id={"head": dest},
            device_id_type=MESH,
        )
        return big, small

    def span(c):
        at = span_at(c)
        load_g(c).wait()
        cb = c_ref[at, :]
        gram = jnp.where(lower, contract(cb, b_ref[at, :], 1, 1), 0.0)
        held = (before_ref[c] + lead_ref[c, 0:1, :] * inc_ref[...]).astype(BF16)
        runT = runT_ref[at, :]
        q = q_ref[:, at]
        hi, lo = halves(jnp.exp2(runT))
        acc = jnp.zeros((SPAN, 128), F32)
        for p in range(width // 128):
            lanes = slice(p * 128, p * 128 + 128)
            xp = x_ref[at, lanes]
            grow = contract(hi, spread16[:, lanes], 1, 0) + contract(lo, spread16[:, lanes], 1, 0)
            carried = contract(cb, held[:, lanes], 1, 0) * grow
            sides = []
            for h in (2 * p, 2 * p + 1):
                m = (
                    gram * jnp.exp2(jnp.minimum(runT[:, h : h + 1] - q[h : h + 1, :], 0.0))
                ).astype(BF16)
                sides.append(jnp.dot(m, xp, preferred_element_type=F32))
            inner = jnp.where(left, sides[0], sides[1])
            z = g_ref[at, lanes].astype(F32)
            skip = jnp.where(left[0:1, :], skip_ref[2 * p], skip_ref[2 * p + 1])
            gated = (inner + carried + skip * xp.astype(F32)) * (
                z * (0.5 * jnp.tanh(0.5 * z) + 0.5)
            )
            acc = acc + gated * gated
            g_ref[at, lanes] = (gated * gain_ref[:, lanes]).astype(BF16)
        ss_buf[c] = contract(ones, acc, 1, 1, HIGH)

    if ranks == 4:
        order = [ranks - 1 - me, lax.rem(me + 2, ranks), me + 1 - 2 * lax.rem(me, 2)]
    else:
        order = [lax.rem(me + k, ranks) for k in range(1, ranks)]
    for index, dest in enumerate(order):
        slot = lax.rem(me - dest + ranks, ranks) - 1

        def one(j, carry, dest=dest, slot=slot):
            span(dest * each + j)
            for copy in copies(dest, j, slot):
                copy.start()
            return carry

        lax.fori_loop(0, each, one, 0)
        if index + 2 < ranks:
            relay(index + 2)

    def mine(j, carry):
        span(me * each + j)
        return carry

    lax.fori_loop(0, each, mine, 0)

    def wait_ws(i, carry):
        load_w(i).wait()
        return carry

    lax.fori_loop(1, shards, wait_ws, 0)
    local = pl.ds(pl.multiple_of(me * share, share), share)

    def own_tile(n, carry):
        lanes = pl.ds(pl.multiple_of(n * TILE, TILE), TILE)
        acc_ref[:, lanes] = jnp.dot(
            g_ref[local, :], w_ref[me, :, lanes], preferred_element_type=F32
        )
        return carry

    lax.fori_loop(0, tiles, own_tile, 0)

    table = near_order(ranks)

    def collect(i):
        r = pick([row[i] for row in table], me)
        slot = lax.rem(r - me + ranks, ranks) - 1

        def pass_on(j, carry):
            landed(r, j).wait_recv()
            across(r, j, core).start()
            return carry

        def wait_across(j, carry):
            across(r, j, 1 - core).wait_recv()
            return carry

        def wait_got(j, carry):
            for copy in copies(r, j, slot):
                copy.wait_recv()
            return carry

        lax.fori_loop(1, chips, pass_on, 0)
        lax.fori_loop(0, chips, wait_across, 0)
        lax.fori_loop(0, each, wait_got, 0)
        return r, slot

    for i in range(ranks - 2):
        r, slot = collect(i)

        def more(n, carry, r=r, slot=slot):
            lanes = pl.ds(pl.multiple_of(n * TILE, TILE), TILE)
            acc_ref[:, lanes] += jnp.dot(
                got_ref[slot], w_ref[r, :, lanes], preferred_element_type=F32
            )
            return carry

        lax.fori_loop(0, tiles, more, 0)

    r, slot = collect(ranks - 2)
    unit = jnp.where(lax.broadcasted_iota(jnp.int32, (8, 128), 0) == 0, 1.0, 0.0).astype(F32)
    scales = []
    for j in range(each):
        total = ss_buf[me * each + j]
        for k in range(ranks - 1):
            total = total + ss_ref[k, j]
        column = contract(total, unit, 0, 0, HIGH) * (1.0 / (width * ranks))
        token = (
            me * share + j * SPAN + lax.broadcasted_iota(jnp.int32, (SPAN, 128), 0)
        )
        scales.append(jnp.where(token < valid, lax.rsqrt(column + 1e-05), 0.0))
    scale = jnp.concatenate(scales, axis=0)

    def put(n):
        lanes = pl.ds(pl.multiple_of(n * TILE, TILE), TILE)
        return pltpu.make_async_copy(res_ref.at[:, lanes], out_hbm.at[:, lanes], out_sem.at[n])

    wide = jnp.concatenate([scale] * (TILE // 128), axis=1)

    def final(n, carry):
        lanes = pl.ds(pl.multiple_of(n * TILE, TILE), TILE)
        part = jnp.dot(got_ref[slot], w_ref[r, :, lanes], preferred_element_type=F32)
        res_ref[:, lanes] = ((acc_ref[:, lanes] + part) * wide).astype(BF16)
        put(n).start()
        return carry

    lax.fori_loop(0, tiles, final, 0)

    for k in range(ranks - 1):
        for step in (1, -1):
            source = me - step * k
            last = me == (ranks - 1 if step > 0 else 0)

            @pl.when((source >= 0) & (source < ranks) & jnp.logical_not(last))
            def _(k=k, step=step):
                along(k, step).wait_send()

    for i in range(ranks - 1):
        r = pick([row[i] for row in table], me)

        def sent_plane(j, carry, r=r):
            plane(r, j).wait_send()
            return carry

        def sent_across(j, carry, r=r):
            across(r, j, core).wait_send()
            return carry

        lax.fori_loop(1, chips, sent_plane, 0)
        lax.fori_loop(0, chips, sent_across, 0)

    def told(j, carry):
        @pl.when(chip + j < chips)
        def _():
            to_chip(j, chip + j).wait_send()

        return carry

    lax.fori_loop(1, chips, told, 0)
    for dest in order:
        slot = lax.rem(me - dest + ranks, ranks) - 1

        def sent(j, carry, dest=dest, slot=slot):
            for copy in copies(dest, j, slot):
                copy.wait_send()
            return carry

        lax.fori_loop(0, each, sent, 0)

    def wait_put(n, carry):
        put(n).wait()
        return carry

    lax.fori_loop(0, tiles, wait_put, 0)


def body(
    ranks,
    shards,
    values,
    gates,
    b_proj,
    c_proj,
    step_size,
    decay_rate,
    skip_gain,
    norm_gain,
    readout,
    span_counts,
    remaining_count,
):
    length, width = values.shape
    heads = step_size.shape[0]
    state = b_proj.shape[1]
    depth = readout.shape[1]
    blocks = length // SPAN
    share = length // ranks
    each = blocks // ranks
    chips = shards // 2
    sds = jax.ShapeDtypeStruct
    smem = pl.BlockSpec(memory_space=pltpu.SMEM)
    hbm = pl.BlockSpec(memory_space=pl.ANY)
    dma = pltpu.SemaphoreType.DMA
    return pl.pallas_call(
        functools.partial(layer_kernel, ranks, shards),
        out_shape=sds((share, depth), BF16),
        in_specs=[smem, smem, smem, pl.BlockSpec(memory_space=VMEM)] + [hbm] * 7,
        out_specs=hbm,
        scratch_shapes=[
            VMEM((length, width), BF16),
            VMEM((length, width), BF16),
            VMEM((length, state), BF16),
            VMEM((length, state), BF16),
            VMEM((heads, length), F32),
            VMEM((heads, length), F32),
            VMEM((length, heads), F32),
            VMEM((heads, length), F32),
            VMEM((blocks, state, width), F32),
            VMEM((blocks, 8, width), F32),
            VMEM((state, width), F32),
            VMEM((8, width), F32),
            VMEM((state + 16, width), BF16),
            VMEM((state + 16, width), BF16),
            VMEM((state + 16, width // 2), BF16),
            VMEM((chips, state + 16, width // 2), BF16),
            VMEM((state, width), F32),
            VMEM((ranks, width, depth), BF16),
            VMEM((ranks - 1, share, width), BF16),
            VMEM((blocks, 8, SPAN), F32),
            VMEM((ranks - 1, each, 8, SPAN), F32),
            VMEM((share, depth), F32),
            VMEM((share, depth), BF16),
            dma((blocks,)),
            dma((blocks,)),
            dma((4,)),
            dma((shards,)),
            dma((ranks - 1,)),
            dma((ranks - 1,)),
            dma((ranks - 1,)),
            dma((ranks - 1,)),
            dma((ranks - 1, chips)),
            dma((ranks - 1, chips)),
            dma((ranks - 1, chips)),
            dma((ranks - 1, chips)),
            dma((2,)),
            dma((2,)),
            dma((chips,)),
            dma((chips,)),
            dma((ranks - 1, each)),
            dma((ranks - 1, each)),
            dma((ranks - 1, each)),
            dma((ranks - 1, each)),
            dma((depth // TILE,)),
        ],
        compiler_params=pltpu.CompilerParams(
            vmem_limit_bytes=LIMIT, collective_id=0, has_side_effects=True
        ),
        cost_estimate=pl.CostEstimate(
            flops=10**11, bytes_accessed=20 * 10**6, transcendentals=0
        ),
        name="layer",
    )(
        span_counts,
        remaining_count,
        skip_gain,
        norm_gain[None, :],
        values,
        gates,
        b_proj,
        c_proj,
        step_size,
        decay_rate,
        readout,
    )


def solution(mesh):
    return jax.shard_map(
        functools.partial(body, mesh.shape["head"], mesh.shape["seq"]),
        mesh=mesh,
        in_specs=(
            P("seq", "head"),
            P("seq", "head"),
            P("seq", None),
            P("seq", None),
            P("head", "seq"),
            P("head", "seq"),
            P("head"),
            P("head"),
            P("head", None),
            P("seq"),
            P("seq"),
        ),
        out_specs=P(("seq", "head"), None),
        check_vma=False,
    )
```

profile of v0, /device:TPU:7, one launch (start us, length us, event | category | flops | bytes accessed | tf_op | source)
XLA Modules:
  0.0 186.6 jit_solution(7766012093528210644)
XLA Ops:
  1.3 1.3 broadcast_in_dim.3.gain_ref
  2.6 180.6 %layer.1 = bf16[512,2560]{1,0:T(8,128)(2,1)} custom-call(s32[1]{0:T(128)S(6)} %copy.13.count_ref, s32[1]{0:T(128)S(6)} %copy.14.remain_ref, f32[20]{0:T(128)} %skip_ref.1, f32[1,1280]{1,0:T(1,128)} %broadcast_in_dim.3.gain_ref, bf16[2048,1280]{1,0:T(8,128)(2,1)} %x_hbm.1, bf16[2048,1280]{1,0:T(8,128)(2,1)} %g_hbm.1, bf16[2048,128]{1,0:T(8,128)(2,1)} %b_hbm.1, ...), custom_call_target="tpu_custom_call" | custom-call | flops 99999997952 | bytes 20000000 | tf_op jit(solution)/shard_map/layer/pallas_call | solution.py:640
  183.2 3.4 %copy.15 = bf16[512,2560]{1,0:T(8,128)(2,1)} copy(bf16[512,2560]{1,0:T(8,128)(2,1)} %layer.1) | data formatting | bytes 5242880
where the time goes:
time: 187 us
  Pallas kernels  181 us (97%)
  local copies, waits for them, and re-layouts  4.69 us (3%)
    pallas_call x1, Pallas kernels, body(): pl.pallas_call(functools.partial(layer_kernel, ranks, shards), out_shape=...  181 us

commit v1 on v0

--- a/solution.py
+++ b/solution.py
@@ -60,6 +60,19 @@
 
 def near_order(ranks):
     return [sorted((r for r in range(ranks) if r != h), key=lambda r: (abs(r - h), r)) for h in range(ranks)]
+
+
+def weight_moves(ranks):
+    if ranks != 4:
+        return [(r, r, t, 0) for r in range(ranks) for t in range(ranks) if t != r]
+    right = [(0, 0, 2, 0), (0, 0, 1, 0), (2, 2, 3, 0), (1, 1, 2, 0), (0, 2, 3, 2), (1, 2, 3, 3)]
+    return right + [(3 - r, 3 - a, 3 - b, phase) for r, a, b, phase in right]
+
+
+def late_order(ranks):
+    if ranks == 4:
+        return [[1, 3, 2], [0, 3, 2], [3, 0, 1], [2, 0, 1]]
+    return near_order(ranks)
 
 
 def layer_kernel(
@@ -104,10 +117,8 @@
     g_sem,
     in_sem,
     w_sem,
-    right_s,
-    right_r,
-    left_s,
-    left_r,
+    along_s,
+    along_r,
     plane_s,
     plane_r,
     sib_s,
@@ -165,33 +176,74 @@
         )
     ]
 
-    def along(k, step):
-        r = me - step * k
-        send, recv = (right_s, right_r) if step > 0 else (left_s, left_r)
+    moves = weight_moves(ranks)
+
+    def along(owner, dest):
         return pltpu.make_async_remote_copy(
-            src_ref=w_ref.at[r, slice_at(place), :],
-            dst_ref=w_ref.at[r, slice_at(place), :],
-            send_sem=send.at[k],
-            recv_sem=recv.at[k],
-            device_id={"head": me + step},
+            src_ref=w_ref.at[owner, slice_at(place), :],
+            dst_ref=w_ref.at[owner, slice_at(place), :],
+            send_sem=along_s.at[owner, dest],
+            recv_sem=along_r.at[owner],
+            device_id={"head": dest},
             device_id_type=MESH,
         )
 
-    def arrived(k, step):
-        r = me - step * (k + 1)
-        send, recv = (right_s, right_r) if step > 0 else (left_s, left_r)
-        return pltpu.make_async_remote_copy(
-            src_ref=w_ref.at[r, slice_at(place), :],
-            dst_ref=w_ref.at[r, slice_at(place), :],
-            send_sem=send.at[k],
-            recv_sem=recv.at[k],
-            device_id={"head": me - step},
-            device_id_type=MESH,
-        )
+    def move(now):
+        for h in range(ranks):
+            mine = [(r, b) for r, a, b, phase in moves if a == h and phase == now]
+            if mine:
+
+                @pl.when(me == h)
+                def _(h=h, mine=mine):
+                    for r, b in mine:
+                        if r != h:
+                            along(r, b).wait_recv()
+                        along(r, b).start()
+
+    def spread_out(early):
+        for h in range(ranks):
+            relayed = [r for r, a, b, phase in moves if a == h and r != h]
+            outer = ranks == 4 and h in (0, ranks - 1)
+            owners = near_order(ranks)[h]
+            if outer:
+                owners = owners[:1] if early else owners[1:]
+            elif not early:
+                owners = []
+            if owners:
+
+                @pl.when(me == h)
+                def _(h=h, relayed=relayed, owners=owners):
+                    for r in owners:
+                        if r not in relayed:
+                            along(r, r).wait_recv()
+                        spread_plane(jnp.int32(r))
+
+    square = chips == 4
+    direct = (1, 2) if square else tuple(range(1, chips))
+
+    def chip_to(j):
+        if square:
+            return (chip, chip + 1 - 2 * lax.rem(chip, 2), lax.rem(chip + 2, 4), 3 - chip)[j]
+        return lax.rem(chip + j, chips)
+
+    def chip_from(j):
+        return chip_to(j) if square else lax.rem(chip - j + chips, chips)
+
+    def over_chips(low, one):
+        if square:
+            for j in range(low, chips):
+                one(j)
+        else:
+
+            def step(j, carry):
+                one(j)
+                return carry
+
+            lax.fori_loop(low, chips, step, 0)
 
     def plane(r, j):
         slot = lax.rem(r - me + ranks, ranks) - 1
-        dest = lax.rem(chip + j, chips) * 2 + core
+        dest = chip_to(j) * 2 + core
         return pltpu.make_async_remote_copy(
             src_ref=w_ref.at[r, slice_at(place), :],
             dst_ref=w_ref.at[r, slice_at(place), :],
@@ -203,7 +255,7 @@
 
     def landed(r, j):
         slot = lax.rem(r - me + ranks, ranks) - 1
-        owner = lax.rem(chip - j + chips, chips) * 2 + core
+        owner = chip_from(j) * 2 + core
         return pltpu.make_async_remote_copy(
             src_ref=w_ref.at[r, slice_at(owner), :],
             dst_ref=w_ref.at[r, slice_at(owner), :],
@@ -213,9 +265,31 @@
             device_id_type=MESH,
         )
 
+    def corner(r, part, dest, owner):
+        slot = lax.rem(r - me + ranks, ranks) - 1
+        low = rows // 32 * 16
+        at = pl.ds(
+            pl.multiple_of((owner * 2 + core) * rows + (low if part else 0), 16),
+            rows - low if part else low,
+        )
+        return pltpu.make_async_remote_copy(
+            src_ref=w_ref.at[r, at, :],
+            dst_ref=w_ref.at[r, at, :],
+            send_sem=plane_s.at[slot, 3 * part],
+            recv_sem=plane_r.at[slot, 3 * part],
+            device_id={"seq": dest * 2 + core},
+            device_id_type=MESH,
+        )
+
+    def turn(r, part):
+        return corner(r, part, chip_to(2 - part), chip_to(1 + part))
+
+    def turned(r, part):
+        return corner(r, part, chip_to(2 - part), chip_to(3))
+
     def across(r, j, of_core):
         slot = lax.rem(r - me + ranks, ranks) - 1
-        owner = lax.rem(chip - j + chips, chips) * 2 + of_core
+        owner = chip_from(j) * 2 + of_core
         return pltpu.make_async_remote_copy(
             src_ref=w_ref.at[r, slice_at(owner), :],
             dst_ref=w_ref.at[r, slice_at(owner), :],
@@ -227,28 +301,11 @@
 
     def spread_plane(r):
         across(r, 0, core).start()
-
-        def one(j, carry):
-            plane(r, j).start()
-            return carry
-
-        lax.fori_loop(1, chips, one, 0)
-
-    def relay(k):
-        for step in (1, -1):
-            source = me - step * k
-            last = me == (ranks - 1 if step > 0 else 0)
-
-            @pl.when((source >= 0) & (source < ranks))
-            def _(step=step, source=source, last=last):
-                arrived(k - 1, step).wait_recv()
-                if k < ranks - 1:
-
-                    @pl.when(jnp.logical_not(last))
-                    def _():
-                        along(k, step).start()
-
-                spread_plane(source)
+        if square:
+            for j in direct:
+                plane(r, j).start()
+        else:
+            over_chips(1, lambda j: plane(r, j).start())
 
     load_w(0).start()
     for copy in smalls[:3]:
@@ -269,25 +326,18 @@
         )
         return carry
 
-    def greet_plane(j, carry):
-        dest = lax.rem(chip + j, chips) * 2 + core
+    def greet_plane(j):
+        dest = chip_to(j) * 2 + core
         pl.semaphore_signal(barrier, inc=1, device_id={"seq": dest}, device_id_type=MESH)
-        return carry
 
     lax.fori_loop(1, ranks, greet, 0)
-    lax.fori_loop(1, chips, greet_plane, 0)
+    over_chips(1, greet_plane)
     pl.semaphore_signal(barrier, inc=1, device_id={"seq": sibling}, device_id_type=MESH)
     pl.semaphore_wait(barrier, ranks - 1 + chips)
 
     load_w(0).wait()
 
-    @pl.when(me < ranks - 1)
-    def _():
-        along(0, 1).start()
-
-    @pl.when(me > 0)
-    def _():
-        along(0, -1).start()
+    move(0)
 
     i0 = lax.broadcasted_iota(jnp.int32, (SPAN, SPAN), 0)
     i1 = lax.broadcasted_iota(jnp.int32, (SPAN, SPAN), 1)
@@ -325,6 +375,7 @@
         return carry
 
     lax.fori_loop(0, blocks, scan, 0)
+    move(1)
     mine_ref[0:state, :] = s_ref[...].astype(BF16)
     mine_ref[state:, :] = pack_rows(l_ref[0:1, :])
 
@@ -372,6 +423,7 @@
         return carry
 
     lax.fori_loop(1, chips, tell, 0)
+    move(2)
     inc_ref[:, cols] = jnp.zeros((state, half), F32)
 
     def hear(i, carry):
@@ -401,7 +453,6 @@
     after = unpack_rows(other_ref[state:, :]) * inc + other_ref[0:state, :].astype(F32)
     inc_ref[...] = jnp.where(core == 1, after, inc)
 
-    relay(1)
     smalls[3].wait()
     left = lax.broadcasted_iota(jnp.int32, (SPAN, 128), 1) < (width // heads)
     ones = jnp.ones((8, 128), F32)
@@ -471,8 +522,9 @@
             return carry
 
         lax.fori_loop(0, each, one, 0)
-        if index + 2 < ranks:
-            relay(index + 2)
+        if index == 0:
+            move(3)
+            spread_out(True)
 
     def mine(j, carry):
         span(me * each + j)
@@ -496,33 +548,54 @@
 
     lax.fori_loop(0, tiles, own_tile, 0)
 
-    table = near_order(ranks)
-
-    def collect(i):
-        r = pick([row[i] for row in table], me)
-        slot = lax.rem(r - me + ranks, ranks) - 1
-
-        def pass_on(j, carry):
-            landed(r, j).wait_recv()
-            across(r, j, core).start()
-            return carry
-
-        def wait_across(j, carry):
-            across(r, j, 1 - core).wait_recv()
-            return carry
-
-        def wait_got(j, carry):
-            for copy in copies(r, j, slot):
-                copy.wait_recv()
-            return carry
-
-        lax.fori_loop(1, chips, pass_on, 0)
-        lax.fori_loop(0, chips, wait_across, 0)
-        lax.fori_loop(0, each, wait_got, 0)
-        return r, slot
+    near = near_order(ranks)
+    late = late_order(ranks)
+
+    def source_of(table, i):
+        return pick([row[i] for row in table], me)
+
+    def pass_direct(i):
+        r = source_of(near, i)
+        if square:
+            for j in direct:
+                landed(r, j).wait_recv()
+                turn(r, j - 1).start()
+                across(r, j, core).start()
+        else:
+
+            def one(j):
+                landed(r, j).wait_recv()
+                across(r, j, core).start()
+
+            over_chips(1, one)
+
+    def pass_corner(i):
+        r = source_of(near, i)
+        if square:
+            for part in (0, 1):
+                turned(r, part).wait_recv()
+            across(r, 3, core).start()
+        over_chips(0, lambda j: across(r, j, 1 - core).wait_recv())
+
+    pass_direct(0)
+    spread_out(False)
+    for i in range(1, ranks - 1):
+        pass_direct(i)
+        pass_corner(i - 1)
+    pass_corner(ranks - 2)
+
+    def take(i):
+        r = source_of(late, i)
+        return r, lax.rem(r - me + ranks, ranks) - 1
+
+    def receive(r, slot, j):
+        for copy in copies(r, j, slot):
+            copy.wait_recv()
 
     for i in range(ranks - 2):
-        r, slot = collect(i)
+        r, slot = take(i)
+        for j in range(each):
+            receive(r, slot, j)
 
         def more(n, carry, r=r, slot=slot):
             lanes = pl.ds(pl.multiple_of(n * TILE, TILE), TILE)
@@ -533,57 +606,53 @@
 
         lax.fori_loop(0, tiles, more, 0)
 
-    r, slot = collect(ranks - 2)
+    r, slot = take(ranks - 2)
     unit = jnp.where(lax.broadcasted_iota(jnp.int32, (8, 128), 0) == 0, 1.0, 0.0).astype(F32)
-    scales = []
+
+    def put(n, j):
+        lanes = pl.ds(pl.multiple_of(n * TILE, TILE), TILE)
+        at = pl.ds(j * SPAN, SPAN)
+        return pltpu.make_async_copy(
+            res_ref.at[at, lanes], out_hbm.at[at, lanes], out_sem.at[n, j]
+        )
+
     for j in range(each):
+        receive(r, slot, j)
         total = ss_buf[me * each + j]
         for k in range(ranks - 1):
             total = total + ss_ref[k, j]
         column = contract(total, unit, 0, 0, HIGH) * (1.0 / (width * ranks))
-        token = (
-            me * share + j * SPAN + lax.broadcasted_iota(jnp.int32, (SPAN, 128), 0)
-        )
-        scales.append(jnp.where(token < valid, lax.rsqrt(column + 1e-05), 0.0))
-    scale = jnp.concatenate(scales, axis=0)
-
-    def put(n):
-        lanes = pl.ds(pl.multiple_of(n * TILE, TILE), TILE)
-        return pltpu.make_async_copy(res_ref.at[:, lanes], out_hbm.at[:, lanes], out_sem.at[n])
-
-    wide = jnp.concatenate([scale] * (TILE // 128), axis=1)
-
-    def final(n, carry):
-        lanes = pl.ds(pl.multiple_of(n * TILE, TILE), TILE)
-        part = jnp.dot(got_ref[slot], w_ref[r, :, lanes], preferred_element_type=F32)
-        res_ref[:, lanes] = ((acc_ref[:, lanes] + part) * wide).astype(BF16)
-        put(n).start()
-        return carry
-
-    lax.fori_loop(0, tiles, final, 0)
-
-    for k in range(ranks - 1):
-        for step in (1, -1):
-            source = me - step * k
-            last = me == (ranks - 1 if step > 0 else 0)
-
-            @pl.when((source >= 0) & (source < ranks) & jnp.logical_not(last))
-            def _(k=k, step=step):
-                along(k, step).wait_send()
+        token = me * share + j * SPAN + lax.broadcasted_iota(jnp.int32, (SPAN, 128), 0)
+        scale = jnp.where(token < valid, lax.rsqrt(column + 1e-05), 0.0)
+        wide = jnp.concatenate([scale] * (TILE // 128), axis=1)
+        at = pl.ds(j * SPAN, SPAN)
+
+        def final(n, carry, j=j, at=at, wide=wide):
+            lanes = pl.ds(pl.multiple_of(n * TILE, TILE), TILE)
+            part = jnp.dot(got_ref[slot, at, :], w_ref[r, :, lanes], preferred_element_type=F32)
+            res_ref[at, lanes] = ((acc_ref[at, lanes] + part) * wide).astype(BF16)
+            put(n, j).start()
+            return carry
+
+        lax.fori_loop(0, tiles, final, 0)
+
+    for h in range(ranks):
+
+        @pl.when(me == h)
+        def _(h=h):
+            for r, a, b, phase in moves:
+                if a == h:
+                    along(r, b).wait_send()
 
     for i in range(ranks - 1):
-        r = pick([row[i] for row in table], me)
-
-        def sent_plane(j, carry, r=r):
-            plane(r, j).wait_send()
-            return carry
-
-        def sent_across(j, carry, r=r):
-            across(r, j, core).wait_send()
-            return carry
-
-        lax.fori_loop(1, chips, sent_plane, 0)
-        lax.fori_loop(0, chips, sent_across, 0)
+        r = source_of(near, i)
+        if square:
+            for j in direct:
+                plane(r, j).wait_send()
+                turn(r, j - 1).wait_send()
+        else:
+            over_chips(1, lambda j: plane(r, j).wait_send())
+        over_chips(0, lambda j: across(r, j, core).wait_send())
 
     def told(j, carry):
         @pl.when(chip + j < chips)
@@ -604,7 +673,8 @@
         lax.fori_loop(0, each, sent, 0)
 
     def wait_put(n, carry):
-        put(n).wait()
+        for j in range(each):
+            put(n, j).wait()
         return carry
 
     lax.fori_loop(0, tiles, wait_put, 0)
@@ -670,10 +740,8 @@
             dma((blocks,)),
             dma((4,)),
             dma((shards,)),
-            dma((ranks - 1,)),
-            dma((ranks - 1,)),
-            dma((ranks - 1,)),
-            dma((ranks - 1,)),
+            dma((ranks, ranks)),
+            dma((ranks,)),
             dma((ranks - 1, chips)),
             dma((ranks - 1, chips)),
             dma((ranks - 1, chips)),
@@ -686,7 +754,7 @@
             dma((ranks - 1, each)),
             dma((ranks - 1, each)),
             dma((ranks - 1, each)),
-            dma((depth // TILE,)),
+            dma((depth // TILE, each)),
         ],
         compiler_params=pltpu.CompilerParams(
             vmem_limit_bytes=LIMIT, collective_id=0, has_side_effects=True

time: 187 us -> 172 us (0.920); the launches traced: 187 us -> 170 us
  Pallas kernels: 181 us -> 164 us
    pallas_call x1, Pallas kernels: 181 us -> 164 us  [body(): pl.pallas_call(functools.partial(layer_kernel, ranks, shards), out_shape=...]
where the time goes in v1:
time: 172 us; the launch traced here: 170 us
  Pallas kernels  164 us (95%)
  local copies, waits for them, and re-layouts  4.69 us (3%)
    pallas_call x1, Pallas kernels, body(): pl.pallas_call(functools.partial(layer_kernel, ranks, shards), out_shape=...  164 us

profile of v1, /device:TPU:7, one launch (start us, length us, event | category | flops | bytes accessed | tf_op | source)
XLA Modules:
  0.0 169.5 jit_solution(4276152108379135711)
XLA Ops:
  1.3 1.3 broadcast_in_dim.3.gain_ref
  2.6 163.5 %layer.1 = bf16[512,2560]{1,0:T(8,128)(2,1)} custom-call(s32[1]{0:T(128)S(6)} %copy.13.count_ref, s32[1]{0:T(128)S(6)} %copy.14.remain_ref, f32[20]{0:T(128)} %skip_ref.1, f32[1,1280]{1,0:T(1,128)} %broadcast_in_dim.3.gain_ref, bf16[2048,1280]{1,0:T(8,128)(2,1)} %x_hbm.1, bf16[2048,1280]{1,0:T(8,128)(2,1)} %g_hbm.1, bf16[2048,128]{1,0:T(8,128)(2,1)} %b_hbm.1, ...), custom_call_target="tpu_custom_call" | custom-call | flops 99999997952 | bytes 20000000 | tf_op jit(solution)/shard_map/layer/pallas_call | solution.py:710
  166.1 3.4 %copy.15 = bf16[512,2560]{1,0:T(8,128)(2,1)} copy(bf16[512,2560]{1,0:T(8,128)(2,1)} %layer.1) | data formatting | bytes 5242880

commit v2 on v1

--- a/solution.py
+++ b/solution.py
@@ -64,9 +64,13 @@
 
 def weight_moves(ranks):
     if ranks != 4:
-        return [(r, r, t, 0) for r in range(ranks) for t in range(ranks) if t != r]
-    right = [(0, 0, 2, 0), (0, 0, 1, 0), (2, 2, 3, 0), (1, 1, 2, 0), (0, 2, 3, 2), (1, 2, 3, 3)]
-    return right + [(3 - r, 3 - a, 3 - b, phase) for r, a, b, phase in right]
+        return [
+            (r, r, t, part, 0) for part in (0, 1) for r in range(ranks) for t in range(ranks) if t != r
+        ]
+    right = [(0, 0, 2, 0, 0), (0, 0, 2, 1, 0), (0, 0, 1, 0, 0), (0, 0, 1, 1, 0)]
+    right += [(2, 2, 3, 0, 0), (2, 2, 3, 1, 0), (1, 1, 2, 0, 0), (1, 1, 2, 1, 0)]
+    right += [(0, 2, 3, 0, 1), (0, 2, 3, 1, 2), (1, 2, 3, 0, 3), (1, 2, 3, 1, 3)]
+    return right + [(3 - r, 3 - a, 3 - b, part, phase) for r, a, b, part, phase in right]
 
 
 def late_order(ranks):
@@ -178,31 +182,35 @@
 
     moves = weight_moves(ranks)
 
-    def along(owner, dest):
+    def along(owner, dest, part):
+        low = rows // 32 * 16
+        at = pl.ds(
+            pl.multiple_of(place * rows + (low if part else 0), 8), rows - low if part else low
+        )
         return pltpu.make_async_remote_copy(
-            src_ref=w_ref.at[owner, slice_at(place), :],
-            dst_ref=w_ref.at[owner, slice_at(place), :],
-            send_sem=along_s.at[owner, dest],
-            recv_sem=along_r.at[owner],
+            src_ref=w_ref.at[owner, at, :],
+            dst_ref=w_ref.at[owner, at, :],
+            send_sem=along_s.at[owner, dest, part],
+            recv_sem=along_r.at[owner, part],
             device_id={"head": dest},
             device_id_type=MESH,
         )
 
     def move(now):
         for h in range(ranks):
-            mine = [(r, b) for r, a, b, phase in moves if a == h and phase == now]
+            mine = [(r, b, part) for r, a, b, part, phase in moves if a == h and phase == now]
             if mine:
 
                 @pl.when(me == h)
                 def _(h=h, mine=mine):
-                    for r, b in mine:
+                    for r, b, part in mine:
                         if r != h:
-                            along(r, b).wait_recv()
-                        along(r, b).start()
+                            along(r, b, part).wait_recv()
+                        along(r, b, part).start()
 
     def spread_out(early):
         for h in range(ranks):
-            relayed = [r for r, a, b, phase in moves if a == h and r != h]
+            relayed = [r for r, a, b, part, phase in moves if a == h and r != h]
             outer = ranks == 4 and h in (0, ranks - 1)
             owners = near_order(ranks)[h]
             if outer:
@@ -215,7 +223,8 @@
                 def _(h=h, relayed=relayed, owners=owners):
                     for r in owners:
                         if r not in relayed:
-                            along(r, r).wait_recv()
+                            for part in (0, 1):
+                                along(r, r, part).wait_recv()
                         spread_plane(jnp.int32(r))
 
     square = chips == 4
@@ -505,7 +514,7 @@
                 z * (0.5 * jnp.tanh(0.5 * z) + 0.5)
             )
             acc = acc + gated * gated
-            g_ref[at, lanes] = (gated * gain_ref[:, lanes]).astype(BF16)
+            g_ref[at, lanes] = (gated * gain_ref[lanes][None, :]).astype(BF16)
         ss_buf[c] = contract(ones, acc, 1, 1, HIGH)
 
     if ranks == 4:
@@ -640,9 +649,9 @@
 
         @pl.when(me == h)
         def _(h=h):
-            for r, a, b, phase in moves:
+            for r, a, b, part, phase in moves:
                 if a == h:
-                    along(r, b).wait_send()
+                    along(r, b, part).wait_send()
 
     for i in range(ranks - 1):
         r = source_of(near, i)
@@ -740,8 +749,8 @@
             dma((blocks,)),
             dma((4,)),
             dma((shards,)),
-            dma((ranks, ranks)),
-            dma((ranks,)),
+            dma((ranks, ranks, 2)),
+            dma((ranks, 2)),
             dma((ranks - 1, chips)),
             dma((ranks - 1, chips)),
             dma((ranks - 1, chips)),
@@ -767,7 +776,7 @@
         span_counts,
         remaining_count,
         skip_gain,
-        norm_gain[None, :],
+        norm_gain,
         values,
         gates,
         b_proj,

time: 172 us -> 169 us (0.983)
  Pallas kernels: 164 us -> 162 us
where the time goes in v2:
time: 169 us; the launch traced here: 167 us
  Pallas kernels  162 us (96%)
  local copies, waits for them, and re-layouts  3.4 us (2%)
    pallas_call x1, Pallas kernels, body(): pl.pallas_call(functools.partial(layer_kernel, ranks, shards), out_shape=...  162 us
    unnamed x1, local copies, waits for them, and re-layouts  3.4 us

profile of v2, /device:TPU:7, one launch (start us, length us, event | category | flops | bytes accessed | tf_op | source)
XLA Modules:
  0.0 166.9 jit_solution(12465367291398134502)
XLA Ops:
  1.3 162.2 %layer.1 = bf16[512,2560]{1,0:T(8,128)(2,1)} custom-call(s32[1]{0:T(128)S(6)} %copy.13.count_ref, s32[1]{0:T(128)S(6)} %copy.14.remain_ref, f32[20]{0:T(128)} %skip_ref.1, f32[1280]{0:T(1024)} %gain_ref.1, bf16[2048,1280]{1,0:T(8,128)(2,1)} %x_hbm.1, bf16[2048,1280]{1,0:T(8,128)(2,1)} %g_hbm.1, bf16[2048,128]{1,0:T(8,128)(2,1)} %b_hbm.1, ...), custom_call_target="tpu_custom_call" | custom-call | flops 99999997952 | bytes 20000000 | tf_op jit(solution)/shard_map/layer/pallas_call | solution.py:719
  163.5 3.4 %copy.15 = bf16[512,2560]{1,0:T(8,128)(2,1)} copy(bf16[512,2560]{1,0:T(8,128)(2,1)} %layer.1) | data formatting | bytes 5242880

commit v3 on v2

--- a/solution.py
+++ b/solution.py
@@ -16,7 +16,7 @@
 MESH = pl.DeviceIdType.MESH
 VMEM = pltpu.VMEM
 LIMIT = 63 * 1024 * 1024
-TILE = 256
+TILE = 512
 
 
 def contract(a, b, da, db, precision=None):
@@ -521,19 +521,21 @@
         order = [ranks - 1 - me, lax.rem(me + 2, ranks), me + 1 - 2 * lax.rem(me, 2)]
     else:
         order = [lax.rem(me + k, ranks) for k in range(1, ranks)]
-    for index, dest in enumerate(order):
-        slot = lax.rem(me - dest + ranks, ranks) - 1
-
-        def one(j, carry, dest=dest, slot=slot):
-            span(dest * each + j)
-            for copy in copies(dest, j, slot):
-                copy.start()
-            return carry
-
-        lax.fori_loop(0, each, one, 0)
-        if index == 0:
-            move(3)
-            spread_out(True)
+    def one(t, carry):
+        j = lax.div(t, ranks - 1)
+        index = lax.rem(t, ranks - 1)
+        dest = jnp.int32(0)
+        for i, value in enumerate(order):
+            dest = dest + jnp.where(index == i, value, 0)
+        span(dest * each + j)
+        for copy in copies(dest, j, lax.rem(me - dest + ranks, ranks) - 1):
+            copy.start()
+        return carry
+
+    lax.fori_loop(0, 2, one, 0)
+    move(3)
+    spread_out(True)
+    lax.fori_loop(2, each * (ranks - 1), one, 0)
 
     def mine(j, carry):
         span(me * each + j)

time: 169 us -> 167 us (0.988)
  Pallas kernels: 162 us -> 159 us
    pallas_call x1, Pallas kernels: 162 us -> 159 us  [body(): pl.pallas_call(functools.partial(layer_kernel, ranks, shards), out_shape=...]
where the time goes in v3:
time: 167 us; the launch traced here: 163 us
  Pallas kernels  159 us (95%)
  local copies, waits for them, and re-layouts  3.4 us (2%)
    pallas_call x1, Pallas kernels, body(): pl.pallas_call(functools.partial(layer_kernel, ranks, shards), out_shape=...  159 us
    unnamed x1, local copies, waits for them, and re-layouts  3.4 us

profile of v3, /device:TPU:7, one launch (start us, length us, event | category | flops | bytes accessed | tf_op | source)
XLA Modules:
  0.0 163.5 jit_solution(1893737487478777442)
XLA Ops:
  1.3 158.8 %layer.1 = bf16[512,2560]{1,0:T(8,128)(2,1)} custom-call(s32[1]{0:T(128)S(6)} %copy.13.count_ref, s32[1]{0:T(128)S(6)} %copy.14.remain_ref, f32[20]{0:T(128)} %skip_ref.1, f32[1280]{0:T(1024)} %gain_ref.1, bf16[2048,1280]{1,0:T(8,128)(2,1)} %x_hbm.1, bf16[2048,1280]{1,0:T(8,128)(2,1)} %g_hbm.1, bf16[2048,128]{1,0:T(8,128)(2,1)} %b_hbm.1, ...), custom_call_target="tpu_custom_call" | custom-call | flops 99999997952 | bytes 20000000 | tf_op jit(solution)/shard_map/layer/pallas_call | solution.py:721
  160.1 3.4 %copy.15 = bf16[512,2560]{1,0:T(8,128)(2,1)} copy(bf16[512,2560]{1,0:T(8,128)(2,1)} %layer.1) | data formatting | bytes 5242880
